TPU v7x, 128 devices: a whole 4x4x4 slice. The times are simulated.
128 devices in a mesh: train: 8 (over z, x_hi), serve: 16 (over x_lo, y, core).
Axes of the slice: x: 4 (x_hi: 2, x_lo: 2; x = x_hi * 2 + x_lo), y: 4, z: 4, core: 2. Of those that a mesh axis runs over, the one named last changes fastest.
Arguments:
- train_weights: bfloat16 [16, 7680, 2112], P(None, 'train', 'serve'), may hold values from -6 to 6
- row_offset: int32 [16, 9], replicated, may hold values from 0 to 7168, as said below
- block_group: int32 [16, 224, 1], P(None, 'train'), may hold values from 0 to 15; in each aligned block of 28 rows (0 to 27, 28 to 55, ..., all dimensions but the last counted through in order) at most 3 rows name the same one
Outputs:
- quant_codes: bfloat16 [16, 16, 8, 3, 32, 2112], P(None, 'serve', 'train')
- block_scales: float32 [16, 16, 8, 3, 2112], P(None, 'serve', 'train')
Inputs may be any that keep to these rules, and one draw needn't show every extreme that they name: For every layer l: row_offset[l, 0] = 0 and row_offset[l, 8] = 7168; every other row_offset[l, t] lies 1 to 32 rows above or below t * 896, never on it; in every layer one entry lies exactly 32 rows above and another exactly 32 rows below; layer 1 has the opposite sign of layer 0 at every such entry. `block_group`: within each aligned block of 28 entries (one training device's blocks of one layer), no group is named more than 3 times; some group reaches 3 in some of them.
All inputs are finite; a program needn't handle non-finite values.
Results may differ from a plain program's by a relative error of at most 0.001.
Values may be sent and summed in bfloat16 or wider, within the bound.
No kernel may reach another device: no remote copies, remote signals or barrier semaphores. Data moves between devices by JAX's collectives and lax.ppermute only.
A program may use at most 128 MiB of HBM per device.

v0:
```python
import jax
import jax.numpy as jnp
from jax import lax
from jax.sharding import Mesh
from jax.sharding import PartitionSpec as P

BLOCK = 32
SHIFT = 32
SERVE = ("serve_0", "serve_1", "serve_2")


def padded_2(cells, sides, width):
    for axis, dim in sides:
        count = lax.axis_size(axis)
        ends = count - 1
        head = lax.slice_in_dim(cells, 0, width, axis=dim)
        tail = lax.slice_in_dim(cells, cells.shape[dim] - width, cells.shape[dim], axis=dim)
        cells = jnp.concatenate(
            [
                lax.ppermute(tail, axis, [(i, (i + 1) % count) for i in range(ends)]),
                cells,
                lax.ppermute(head, axis, [((i + 1) % count, i) for i in range(ends)]),
            ],
            axis=dim,
        )
    return cells


def cut_along(value, dim, peers):
    lengths = value.shape
    pieces = value.reshape(*lengths[:dim], peers, lengths[dim] // peers, *lengths[dim + 1 :])
    return jnp.moveaxis(pieces, dim, 0)


def joined_along(pieces, dim):
    lengths = list(pieces.shape[1:])
    lengths[dim] *= pieces.shape[0]
    return jnp.moveaxis(pieces, 0, dim).reshape(lengths)


def turned_blocks(pieces, axes, sequence):
    inside = pieces.shape[1:]
    out = pieces.reshape(*(lax.axis_size(a) for a in axes), *inside)
    for k in sequence:
        out = lax.all_to_all(out, axes[k], k, k, tiled=True)
    return out.reshape(-1, *inside)


def two_step_exchange(value, groups, sequence, split_dim, concat_dim):
    peers = lax.axis_size(groups[0]) * lax.axis_size(groups[1])
    pieces = cut_along(value, split_dim, peers)
    return joined_along(turned_blocks(pieces, groups, sequence), concat_dim)


def shards(train_weights, row_offset, block_group):
    train_n = lax.axis_size("train")
    serve_n = lax.axis_size(SERVE)
    train_idx = lax.axis_index("train")
    buffer_len = train_weights.shape[1]
    rows_dev = buffer_len - 2 * SHIFT
    blocks_dev = block_group.shape[1]
    slots_n = (blocks_dev + serve_n - 1) // serve_n + 1
    entries = jnp.arange(train_n + 1, dtype=jnp.int32)
    position = jnp.arange(blocks_dev, dtype=jnp.int32)
    earlier = position[None, :] < position[:, None]
    slot_range = jnp.arange(serve_n * slots_n, dtype=jnp.int32)
    group_ids = block_group[:, :, 0]
    layer_count = train_weights.shape[0]
    columns = train_weights.shape[2]
    first_row = (
        jnp.sum(jnp.where(entries[None, :] == train_idx, row_offset, 0), axis=1)
        - train_idx * rows_dev
    )
    next_row = (
        jnp.sum(jnp.where(entries[None, :] == train_idx + 1, row_offset, 0), axis=1)
        - train_idx * rows_dev
    )
    padded = padded_2(train_weights, (("train", 1),), SHIFT)
    left_rows = padded[:, :SHIFT]
    right_rows = padded[:, SHIFT + buffer_len :]
    own_rows = padded[:, 2 * SHIFT : 2 * SHIFT + rows_dev]
    filler = jnp.zeros((layer_count, rows_dev - SHIFT, columns), train_weights.dtype)
    left_full = jnp.concatenate([left_rows, filler], axis=1)
    right_full = jnp.concatenate([filler, right_rows], axis=1)
    row_pos = jnp.arange(rows_dev, dtype=jnp.int32)[None, :, None]
    joined = jnp.where(
        row_pos < first_row[:, None, None],
        left_full,
        jnp.where(row_pos >= next_row[:, None, None], right_full, own_rows),
    )
    blocks = joined.reshape(layer_count, blocks_dev, BLOCK, columns)
    same_group = group_ids[:, :, None] == group_ids[:, None, :]
    order_in = jnp.sum((same_group & earlier[None]).astype(jnp.int32), axis=2)
    slot_id = group_ids * slots_n + order_in
    onehot = slot_id[:, None, :] == slot_range[None, :, None]
    absmax = jnp.max(jnp.abs(blocks.astype(jnp.float32)), axis=2, keepdims=True)
    divisor = jnp.maximum(absmax, 0.25)
    coded = (blocks.astype(jnp.float32) / divisor).astype(jnp.bfloat16)
    codes_sent = jnp.einsum(
        "gqj,gjrc->gqrc", onehot.astype(jnp.bfloat16), coded, preferred_element_type=jnp.float32
    ).astype(jnp.bfloat16)
    codes_sent = codes_sent.reshape(layer_count, serve_n, slots_n, BLOCK, columns)
    scale_sent = jnp.einsum(
        "gqj,gjrc->gqrc", onehot.astype(jnp.float32), divisor, precision=lax.Precision.HIGHEST
    )
    scale_sent = scale_sent.reshape(layer_count, serve_n, slots_n, 1, columns)
    quant_codes = two_step_exchange(codes_sent, (("serve_0", "serve_1"), "serve_2"), (1, 0), 1, 4)
    block_scale = lax.all_to_all(scale_sent, SERVE, split_axis=1, concat_axis=4, tiled=True)
    return (
        quant_codes.reshape(layer_count, 1, 1, slots_n, BLOCK, -1),
        block_scale.reshape(layer_count, 1, 1, slots_n, -1),
    )


def solution(mesh):
    finer = Mesh(
        mesh.devices.reshape(mesh.shape["train"], 2, 4, 2),
        ("train", "serve_0", "serve_1", "serve_2"),
    )
    placed = (P(None, "train", SERVE), P(), P(None, "train", None))
    return jax.shard_map(
        shards,
        mesh=finer,
        in_specs=placed,
        out_specs=(P(None, SERVE, "train", None, None, None), P(None, SERVE, "train", None, None)),
        check_vma=False,
    )
```

profile of v0, /device:TPU:38, one launch (start us, length us, event | category | flops | bytes accessed | tf_op | source)
XLA Modules:
  0.0 290.1 jit_solution(9552514334235077035)
XLA Ops:
  0.6 1.5 fusion.12
  2.1 0.5 copy.83
  2.6 3.3 %collective-permute-start.1 = (bf16[16,32,132]{2,1,0:T(8,128)(2,1)S(1)}, bf16[16,32,132]{2,1,0:T(8,128)(2,1)S(1)}, u32[]{:S(2)}, u32[]{:S(2)}) collective-permute-start(bf16[16,32,132]{2,1,0:T(8,128)(2,1)S(1)} %copy.83), channel_id=1, source_target_pairs={{16,0},{32,16},{48,32},{64,48},{80,64},{96,80},{112,96},{17,1},{33... | collective-permute-start | bytes 405512 | tf_op jit(solution)/shard_map/ppermute | solution.py:22
  6.0 0.5 copy.82
  6.5 4.9 %collective-permute-start = (bf16[16,32,132]{2,1,0:T(8,128)(2,1)S(1)}, bf16[16,32,132]{2,1,0:T(8,128)(2,1)S(1)}, u32[]{:S(2)}, u32[]{:S(2)}) collective-permute-start(bf16[16,32,132]{2,1,0:T(8,128)(2,1)S(1)} %copy.82), channel_id=1, source_target_pairs={{0,16},{16,32},{32,48},{48,64},{64,80},{80,96},{96,112},{1,17},{17... | collective-permute-start | bytes 405512 | tf_op jit(solution)/shard_map/ppermute | solution.py:20
  11.4 6.1 %slice.11 = bf16[16,896,132]{1,0,2:T(8,128)(2,1)} slice(bf16[16,960,132]{1,0,2:T(8,128)(2,1)} %param.3), slice={[0:16], [32:928], [0:132]} | slice | bytes 7569408 | tf_op jit(solution)/shard_map/slice | solution.py:81
  17.6 0.1 select_reduce_fusion.1
  17.7 0.1 iota_compare_fusion.2
  17.8 0.1 copy.61
  17.9 0.6 convert_reduce_fusion
  18.6 11.7 %copy.84 = bf16[16,896,132]{2,1,0:T(8,128)(2,1)} copy(bf16[16,896,132]{1,0,2:T(8,128)(2,1)} %slice.11) | data formatting | bytes 7569408
  30.4 0.1 iota_compare_fusion.3
  30.5 6.4 %select_select_fusion = bf16[16,896,132]{2,1,0:T(8,128)(2,1)S(1)} fusion(bf16[16,896,132]{2,1,0:T(8,128)(2,1)} %copy.84, bf16[16,32,132]{2,1,0:T(8,128)(2,1)S(1)} %collective-permute-done.1, bf16[16,32,132]{2,1,0:T(8,128)(2,1)S(1)} %collective-permute-done, pred[16,896]{1,0:T(8,128)(4,1)S(1)} %iota_compare_fusion.2, pred[16,896]{1,0:T(8,128)(4,1)S(1)} %iota_compare_fusion.3), kind=kLoop, calls=%fused_computation.6 | loop fusion | flops 3784704 | bytes 7868416 | tf_op jit(solution)/shard_map/jit(_where)/select_n | solution.py:86
  36.9 4.1 %fusion = f32[16,28,132]{2,1,0:T(8,128)S(1)} fusion(bf16[16,28,32,132]{3,2,1,0:T(8,128)(2,1)S(1)} %bitcast.35), kind=kLoop, calls=%fused_computation.2 | loop fusion | flops 5617920 | bytes 4021248 | tf_op jit(solution)/shard_map/reduce_max | solution.py:96
  41.0 0.8 broadcast_maximum_fusion
  41.9 7.3 %fusion.1 = bf16[16,28,32,132]{3,2,1,0:T(8,128)(2,1)} fusion(bf16[16,28,32,132]{3,2,1,0:T(8,128)(2,1)S(1)} %bitcast.36, f32[16,28,132]{2,1,0:T(8,128)} %broadcast_maximum_fusion), kind=kLoop, calls=%fused_computation.3 | loop fusion | flops 5677056 | bytes 7805952 | tf_op jit(solution)/shard_map/convert_element_type | solution.py:98
  49.1 0.7 fusion.7
  49.9 1.3 copy.73
  51.2 12.7 %fusion.4 = bf16[16,48,32,132]{3,1,2,0:T(8,128)(2,1)} fusion(bf16[16,28,32,132]{3,2,1,0:T(8,128)(2,1)} %fusion.1, s32[16,28]{1,0:T(8,128)S(1)} %copy.63), kind=kOutput, calls=%fused_computation.7 | convolution fusion | flops 184931328 | bytes 10274560 | tf_op jit(solution)/shard_map/gqj,gjrc->gqrc/dot_general | solution.py:99
  63.9 9.0 %copy.68 = bf16[16,48,32,132]{3,2,1,0:T(8,128)(2,1)S(1)} copy(bf16[16,48,32,132]{3,1,2,0:T(8,128)(2,1)} %fusion.4) | data formatting | bytes 12976128 | tf_op jit(solution)/shard_map/convert_element_type | solution.py:101
  72.9 1.9 copy.69
  74.9 15.4 %all_to_all.25 = bf16[8,2,16,1,3,32,132]{6,5,4,0,2,3,1:T(8,128)(2,1)} all-to-all(bf16[8,2,16,1,3,32,132]{6,5,4,0,2,3,1:T(8,128)(2,1)S(1)} %copy.69), channel_id=1, replica_groups=mesh['train'=8,'serve_0'=2,'serve_1'=4,'serve_2'=2] {'serve_2'}, dimensions={1} | all-to-all | bytes 12976128 | tf_op jit(solution)/shard_map/all_to_all | solution.py:45
  90.3 6.0 %all-to-all-start.2 = ((f32[16,16,3,1,132]{4,0,2,3,1:T(8,128)}), f32[16,16,3,1,132]{4,0,2,3,1:T(8,128)S(1)}, u32[]{:S(2)}, u32[]{:S(2)}) async-start(f32[16,16,3,1,132]{4,0,2,3,1:T(8,128)} %bitcast.13), calls=%async_computation.2 | async-start | bytes 1572864 | tf_op jit(solution)/shard_map/all_to_all | solution.py:108
  96.3 10.9 %copy.70 = bf16[8,2,16,1,3,32,132]{6,5,4,1,2,3,0:T(8,128)(2,1)} copy(bf16[8,2,16,1,3,32,132]{6,5,4,0,2,3,1:T(8,128)(2,1)} %all_to_all.25) | data formatting | bytes 12976128 | tf_op jit(solution)/shard_map/all_to_all | solution.py:45
  107.2 1.4 all-to-all-done.2
  108.6 6.8 %all-to-all-start.1 = ((bf16[8,2,16,1,3,32,132]{6,5,4,1,2,3,0:T(8,128)(2,1)}), bf16[8,2,16,1,3,32,132]{6,5,4,1,2,3,0:T(8,128)(2,1)}, u32[]{:S(2)}, u32[]{:S(2)}) async-start(bf16[8,2,16,1,3,32,132]{6,5,4,1,2,3,0:T(8,128)(2,1)} %copy.70), calls=%async_computation.1 | async-start | bytes 25165824 | tf_op jit(solution)/shard_map/all_to_all | solution.py:45
  115.4 0.5 copy.80
  115.8 1.9 reshape.118
  117.7 135.3 %all-to-all-done.1 = bf16[8,2,16,1,3,32,132]{6,5,4,1,2,3,0:T(8,128)(2,1)} async-done(((bf16[8,2,16,1,3,32,132]{6,5,4,1,2,3,0:T(8,128)(2,1)}), bf16[8,2,16,1,3,32,132]{6,5,4,1,2,3,0:T(8,128)(2,1)}, u32[]{:S(2)}, u32[]{:S(2)}) %all-to-all-start.1) | async-done | bytes 6488096 | tf_op jit(solution)/shard_map/all_to_all | solution.py:45
  253.0 6.3 %copy.71 = bf16[8,2,16,1,3,32,132]{6,5,4,2,1,0,3:T(8,128)(2,1)S(1)} copy(bf16[8,2,16,1,3,32,132]{6,5,4,1,2,3,0:T(8,128)(2,1)} %all-to-all-done.1) | data formatting | bytes 12976128 | tf_op jit(solution)/shard_map/all_to_all | solution.py:45
  259.3 9.7 %copy.72 = bf16[16,1,3,32,16,132]{5,4,3,2,0,1:T(8,128)(2,1)} copy(bf16[16,1,3,32,16,132]{5,3,2,0,4,1:T(8,128)(2,1)S(1)} %bitcast.38) | data formatting | bytes 12976128 | tf_op jit(solution)/shard_map/transpose | solution.py:38
  269.0 21.1 %reshape_reshape.7 = bf16[16,1,1,3,32,2112]{5,4,3,0,2,1:T(8,128)(2,1)} reshape(bf16[16,1,3,32,16,132]{5,4,3,2,0,1:T(8,128)(2,1)} %copy.72) | data formatting | bytes 12976128 | tf_op jit(solution)/shard_map/reshape;reshape | solution.py:110
  (12 shorter events, 0.1 us)
Async XLA Ops:
  0.6 16.9 %copy-start.1 = (s32[16,9]{1,0:T(8,128)S(1)}, s32[16,9]{1,0:T(8,128)}, u32[]{:S(2)}) copy-start(s32[16,9]{1,0:T(8,128)} %param.4) | copy-start | bytes 1732
  0.6 17.2 %copy-start = (s32[16,28,1]{1,2,0:T(1,128)S(1)}, s32[16,28,1]{1,2,0:T(1,128)}, u32[]{:S(2)}) copy-start(s32[16,28,1]{1,2,0:T(1,128)} %param.5) | copy-start | bytes 5380
  2.6 27.8 %collective-permute-start.1 = (bf16[16,32,132]{2,1,0:T(8,128)(2,1)S(1)}, bf16[16,32,132]{2,1,0:T(8,128)(2,1)S(1)}, u32[]{:S(2)}, u32[]{:S(2)}) collective-permute-start(bf16[16,32,132]{2,1,0:T(8,128)(2,1)S(1)} %copy.83), channel_id=1, source_target_pairs={{16,0},{32,16},{48,32},{64,48},{80,64},{96,80},{112,96},{17,1},{33... | collective-permute-start | bytes 405512 | tf_op jit(solution)/shard_map/ppermute | solution.py:22
  6.5 24.0 %collective-permute-start = (bf16[16,32,132]{2,1,0:T(8,128)(2,1)S(1)}, bf16[16,32,132]{2,1,0:T(8,128)(2,1)S(1)}, u32[]{:S(2)}, u32[]{:S(2)}) collective-permute-start(bf16[16,32,132]{2,1,0:T(8,128)(2,1)S(1)} %copy.82), channel_id=1, source_target_pairs={{0,16},{16,32},{32,48},{48,64},{64,80},{80,96},{96,112},{1,17},{17... | collective-permute-start | bytes 405512 | tf_op jit(solution)/shard_map/ppermute | solution.py:20
  90.3 18.3 %all-to-all-start.2 = ((f32[16,16,3,1,132]{4,0,2,3,1:T(8,128)}), f32[16,16,3,1,132]{4,0,2,3,1:T(8,128)S(1)}, u32[]{:S(2)}, u32[]{:S(2)}) async-start(f32[16,16,3,1,132]{4,0,2,3,1:T(8,128)} %bitcast.13), calls=%async_computation.2 | async-start | bytes 1572864 | tf_op jit(solution)/shard_map/all_to_all | solution.py:108
  108.6 144.4 %all-to-all-start.1 = ((bf16[8,2,16,1,3,32,132]{6,5,4,1,2,3,0:T(8,128)(2,1)}), bf16[8,2,16,1,3,32,132]{6,5,4,1,2,3,0:T(8,128)(2,1)}, u32[]{:S(2)}, u32[]{:S(2)}) async-start(bf16[8,2,16,1,3,32,132]{6,5,4,1,2,3,0:T(8,128)(2,1)} %copy.70), calls=%async_computation.1 | async-start | bytes 25165824 | tf_op jit(solution)/shard_map/all_to_all | solution.py:45
where the time goes:
time: 292 us; the launch traced here: 290 us
  waiting for transfers between devices  137 us (47%)
  local copies, waits for them, and re-layouts  83.2 us (28%)
  starting transfers between devices  21 us (7%)
  other arithmetic  19.6 us (7%)
  blocking collectives  15.4 us (5%)
  matrix products  13.4 us (5%)
    all_to_all x1, waiting for transfers between devices, turned_blocks(): out = lax.all_to_all(out, axes[k], k, k, tiled=True)  135 us
    another operation x1, local copies, waits for them, and re-layouts, shards(): quant_codes.reshape(layer_count, 1, 1, slots_n, BLOCK, -1)  21.1 us
    all_to_all x2, local copies, waits for them, and re-layouts, turned_blocks(): out = lax.all_to_all(out, axes[k], k, k, tiled=True)  17.2 us
    all_to_all x1, blocking collectives, turned_blocks(): out = lax.all_to_all(out, axes[k], k, k, tiled=True)  15.4 us
    unnamed x10, local copies, waits for them, and re-layouts  15.2 us
    dot_general x1, matrix products, shards(): jnp.einsum('gqj,gjrc->gqrc', onehot.astype(jnp.bfloat16), coded, preferre...  12.7 us
    transpose x1, local copies, waits for them, and re-layouts, joined_along(): return jnp.moveaxis(pieces, 0, dim).reshape(lengths)  9.73 us
    convert_element_type x1, local copies, waits for them, and re-layouts, shards(): codes_sent = jnp.einsum('gqj,gjrc->gqrc', onehot.astype(jnp.bfloat16), co...  9 us
  transfers between devices with their start and end apart: 4, of which 2 were waited for; matrix products, arithmetic and copies ran while one was open for 11% of the time, Pallas kernels for 0%

commit v1 on v0

v1 whole, which is shorter than its diff:
```python
import functools

import jax
import jax.numpy as jnp
from jax import lax
from jax.experimental import pallas as pl
from jax.experimental.pallas import tpu as pltpu
from jax.sharding import PartitionSpec as P

BLOCK = 32
SHIFT = 32
LANES = 128
PACK = 16
NT = (((1,), (1,)), ((), ()))
F32 = jnp.float32
BF16 = jnp.bfloat16
MIB = 1024 * 1024


def iota(shape, dim):
    return lax.broadcasted_iota(jnp.int32, shape, dim)


def identity(n):
    return (iota((n, n), 0) == iota((n, n), 1)).astype(BF16)


def layer_major():
    out, src = iota((PACK * PACK, PACK * PACK), 0), iota((PACK * PACK, PACK * PACK), 1)
    return ((out // PACK == src % PACK) & (out % PACK == src // PACK)).astype(BF16)


def spread(layer):
    src, lane = iota((4 * PACK, LANES), 0), iota((4 * PACK, LANES), 1)
    return ((src % PACK == layer) & (src // PACK == lane % 4)).astype(BF16)


def dot(a, b):
    return jnp.dot(a, b, preferred_element_type=F32)


def edges_kernel(me_ref, first_ref, last_ref, head_ref, tail_ref, planes):
    rows = 2 * SHIFT
    lane = iota((1, 1, LANES), 2)
    perm = layer_major()
    eye = (iota((rows, LANES), 0) == iota((rows, LANES), 1)).astype(BF16)
    zero = jnp.zeros((), BF16)

    def columns(start, count):
        first, last = first_ref[pl.ds(start, count)], last_ref[pl.ds(start, count)]
        return jnp.where(lane < SHIFT, first, jnp.where(lane < rows, last, zero))

    for i in range(LANES // PACK):
        x = columns(PACK * i, PACK).reshape(PACK * PACK, LANES)
        planes[:, PACK * i : PACK * (i + 1), :] = dot(perm, x).astype(BF16).reshape(PACK, PACK, LANES)
    shift = 4 * me_ref[0]
    for layer in range(PACK):
        turned = lax.dot_general(eye, planes[layer], NT, preferred_element_type=F32)
        turned = pltpu.roll(turned, shift, 1).astype(BF16)
        head_ref[layer], tail_ref[layer] = turned[:SHIFT], turned[SHIFT:]
    rest = columns(LANES, 4).reshape(4 * PACK, LANES)
    rest = jnp.concatenate([rest, jnp.zeros_like(rest)], axis=0)
    turned = lax.dot_general(eye, rest, NT, preferred_element_type=F32).astype(BF16)
    head_ref[PACK], tail_ref[PACK] = turned[:SHIFT], turned[SHIFT:]


def turn_kernel(me_ref, x_hbm, rows_ref, rest_ref, x_ref, planes, sems):
    length = x_ref.shape[2]
    steps = LANES // PACK
    parts = [pl.ds(PACK * i, PACK) for i in range(steps)] + [pl.ds(LANES, 4)]
    copies = [pltpu.make_async_copy(x_hbm.at[p], x_ref.at[p], sems.at[i]) for i, p in enumerate(parts)]
    for copy in copies:
        copy.start()
    perm = layer_major()
    for i in range(steps):
        copies[i].wait()
        x = x_ref[parts[i]].reshape(PACK * PACK, length)
        planes[:, PACK * i : PACK * (i + 1), :] = dot(perm, x).astype(BF16).reshape(PACK, PACK, length)
    copies[steps].wait()
    rest = x_ref[parts[steps]].reshape(4 * PACK, length)
    cuts = [(start, min(256, length - start)) for start in range(0, length, 256)]
    for start, size in cuts:
        rest_ref[start : start + size, :] = lax.dot_general(
            identity(size), rest[:, start : start + size], NT, preferred_element_type=F32
        ).astype(BF16)
    shift = 4 * me_ref[0]

    def layer_step(layer, carry):
        for start, size in cuts:
            turned = lax.dot_general(
                identity(size), planes[layer, :, start : start + size], NT, preferred_element_type=F32
            )
            rows_ref[layer, start : start + size, :] = pltpu.roll(turned, shift, 1).astype(BF16)
        return carry

    lax.fori_loop(0, PACK, layer_step, 0)


def pack_kernel(
    slots, me_ref, first_ref, next_ref, group_ref, rows_ref, rest_ref, left_ref, right_ref, out_ref, extra, count
):
    layers, blocks = group_ref.shape
    length = rest_ref.shape[0]
    row = iota((BLOCK, LANES), 0)
    lane_group = iota((BLOCK, LANES), 1) // 4
    me = me_ref[0]
    for g in range(out_ref.shape[0]):
        count[g] = 0

    def layer_step(layer, carry):
        repeat = spread(layer)
        extra[:length] = dot(rest_ref[...], repeat).astype(BF16)
        first, after = first_ref[layer], next_ref[layer] - (blocks - 1) * BLOCK
        left_rest = dot(left_ref[layers][:, : 4 * PACK], repeat).astype(BF16)
        right_rest = dot(right_ref[layers][:, : 4 * PACK], repeat).astype(BF16)
        for b in range(blocks):
            at = SHIFT + BLOCK * b
            block = rows_ref[layer, at : at + BLOCK, :]
            rest = extra[at : at + BLOCK, :]
            if b == 0:
                block = jnp.where(row < first, left_ref[layer], block)
                rest = jnp.where(row < first, left_rest, rest)
            if b == blocks - 1:
                block = jnp.where(row >= after, right_ref[layer], block)
                rest = jnp.where(row >= after, right_rest, rest)
            group = group_ref[layer, b]
            j = count[group]
            count[group] = j + 1
            out_ref[group, j] = block
            tile = slots + lax.shift_right_logical(j, 5)
            place = (j + me) & 31
            out_ref[group, tile] = jnp.where(lane_group == place, rest, out_ref[group, tile])
        return carry

    lax.fori_loop(0, layers, layer_step, 0)


def join_kernel(slots, base_ref, used_ref, in_hbm, codes_ref, scale_ref, held, sems):
    peers, units = in_hbm.shape[0], in_hbm.shape[1]
    per_layer = codes_ref.shape[1]
    layer = pl.program_id(0)
    cuts = [(slots, units - slots)] + [(start, min(8, slots - start)) for start in range(0, slots, 8)]
    copies = [
        pltpu.make_async_copy(in_hbm.at[:, pl.ds(s, n)], held.at[:, pl.ds(s, n)], sems.at[i])
        for i, (s, n) in enumerate(cuts)
    ]

    @pl.when(layer == 0)
    def _():
        for copy in copies:
            copy.start()
        copies[0].wait()

    for i in range(1, len(copies)):
        @pl.when(layer == cuts[i][0] // per_layer)
        def _(i=i):
            copies[i].wait()

    lane = iota((BLOCK, LANES), 1)
    base, used = base_ref[layer], used_ref[layer]
    width = codes_ref.shape[3]
    for k in range(per_layer):

        @pl.when(k < used)
        def _(k=k):
            j = base + k
            tile = slots + lax.shift_right_logical(j, 5)
            jj = j & 31
            source = (lane // 4 - jj) & 31
            rest = jnp.zeros((BLOCK, LANES), F32)
            for s in range(peers):
                rest = jnp.where(source == s, held[s, tile].astype(F32), rest)
            rest = pltpu.roll(rest, (LANES - 4 * jj) & (LANES - 1), 1)
            before = None
            for t in range(peers + 1):
                x = rest
                if before is not None:
                    x = jnp.where(lane < 4 * t - 4, before, x)
                if t < peers:
                    own = held[t, j].astype(F32)
                    x = own if t == 0 else jnp.where(lane >= 4 * t, own, x)
                    before = own
                size = min(LANES, width - LANES * t)
                top = jnp.maximum(jnp.max(jnp.abs(x), axis=0, keepdims=True), 0.25)
                scale_ref[k, :, LANES * t : LANES * t + size] = top[:, :size]
                code = (x * (1.0 / top)).astype(BF16)
                codes_ref[0, k, :, LANES * t : LANES * t + size] = code[:, :size]

        @pl.when(k >= used)
        def _(k=k):
            codes_ref[0, k] = jnp.zeros((BLOCK, width), BF16)
            scale_ref[k] = jnp.zeros((1, width), F32)


def in_vmem():
    return pl.BlockSpec(memory_space=pltpu.VMEM)


def in_smem():
    return pl.BlockSpec(memory_space=pltpu.SMEM)


def shards(train_weights, row_offset, block_group):
    train_n = lax.axis_size("train")
    serve_n = lax.axis_size("serve")
    train_idx = lax.axis_index("train")
    serve_idx = lax.axis_index("serve").astype(jnp.int32)
    layers, buffer_len, columns = train_weights.shape
    rows_dev = buffer_len - 2 * SHIFT
    blocks_dev = block_group.shape[1]
    per_layer = (blocks_dev + serve_n - 1) // serve_n + 1
    slots = layers * per_layer
    units = slots + -(-slots // 32)
    width = columns * serve_n
    groups = block_group[:, :, 0]
    me = serve_idx.reshape(1)
    by_column = jnp.transpose(train_weights, (2, 0, 1))

    tile = (columns, layers, LANES)
    edge = jax.ShapeDtypeStruct((layers + 1, SHIFT, LANES), BF16)
    head, tail = pl.pallas_call(
        edges_kernel,
        grid=(1,),
        in_specs=[
            in_smem(),
            pl.BlockSpec(tile, lambda i: (0, 0, 0)),
            pl.BlockSpec(tile, lambda i: (0, 0, (buffer_len - 2 * SHIFT) // LANES)),
        ],
        out_specs=[in_vmem(), in_vmem()],
        out_shape=[edge, edge],
        scratch_shapes=[pltpu.VMEM((layers, LANES, LANES), BF16)],
        compiler_params=pltpu.CompilerParams(vmem_limit_bytes=16 * MIB),
        cost_estimate=pl.CostEstimate(flops=10**8, bytes_accessed=10**6, transcendentals=0),
        name="edges",
    )(me, by_column, by_column)
    left = lax.ppermute(tail, "train", [(i, i + 1) for i in range(train_n - 1)])
    right = lax.ppermute(head, "train", [(i + 1, i) for i in range(train_n - 1)])

    rows, rest = pl.pallas_call(
        turn_kernel,
        in_specs=[in_smem(), pl.BlockSpec(memory_space=pl.ANY)],
        out_specs=[in_vmem(), in_vmem()],
        out_shape=[
            jax.ShapeDtypeStruct((layers, buffer_len, LANES), BF16),
            jax.ShapeDtypeStruct((buffer_len, 4 * PACK), BF16),
        ],
        scratch_shapes=[
            pltpu.VMEM((columns, layers, buffer_len), BF16),
            pltpu.VMEM((layers, LANES, buffer_len), BF16),
            pltpu.SemaphoreType.DMA((LANES // PACK + 1,)),
        ],
        compiler_params=pltpu.CompilerParams(vmem_limit_bytes=32 * MIB),
        cost_estimate=pl.CostEstimate(flops=3 * 10**9, bytes_accessed=9 * 10**6, transcendentals=0),
        name="turn",
    )(me, by_column)

    entries = jnp.arange(train_n + 1, dtype=jnp.int32)
    first_row = jnp.sum(jnp.where(entries[None, :] == train_idx, row_offset, 0), axis=1) - train_idx * rows_dev
    next_row = jnp.sum(jnp.where(entries[None, :] == train_idx + 1, row_offset, 0), axis=1) - train_idx * rows_dev
    sent = pl.pallas_call(
        functools.partial(pack_kernel, slots),
        in_specs=[in_smem()] * 4 + [in_vmem()] * 4,
        out_specs=in_vmem(),
        out_shape=jax.ShapeDtypeStruct((serve_n, units, BLOCK, LANES), BF16),
        scratch_shapes=[pltpu.VMEM((buffer_len, LANES), BF16), pltpu.SMEM((serve_n,), jnp.int32)],
        compiler_params=pltpu.CompilerParams(vmem_limit_bytes=24 * MIB),
        cost_estimate=pl.CostEstimate(flops=10**9, bytes_accessed=10**7, transcendentals=0),
        name="pack",
    )(me, first_row, next_row, groups, rows, rest, left, right)

    got = lax.all_to_all(sent, "serve", split_axis=0, concat_axis=0, tiled=True)

    used = jnp.sum((groups == serve_idx).astype(jnp.int32), axis=1)
    order = jnp.arange(layers, dtype=jnp.int32)
    base = jnp.sum(jnp.where(order[None, :] < order[:, None], used[None, :], 0), axis=1)
    codes, scales = pl.pallas_call(
        functools.partial(join_kernel, slots),
        grid=(layers,),
        in_specs=[in_smem(), in_smem(), pl.BlockSpec(memory_space=pl.ANY)],
        out_specs=[
            pl.BlockSpec((1, per_layer, BLOCK, width), lambda i: (i, 0, 0, 0)),
            pl.BlockSpec((per_layer, 1, width), lambda i: (i, 0, 0)),
        ],
        out_shape=[
            jax.ShapeDtypeStruct((layers, per_layer, BLOCK, width), BF16),
            jax.ShapeDtypeStruct((layers * per_layer, 1, width), F32),
        ],
        scratch_shapes=[
            pltpu.VMEM((serve_n, units, BLOCK, LANES), BF16),
            pltpu.SemaphoreType.DMA((1 + -(-slots // 8),)),
        ],
        compiler_params=pltpu.CompilerParams(
            dimension_semantics=("arbitrary",), vmem_limit_bytes=24 * MIB
        ),
        cost_estimate=pl.CostEstimate(flops=10**8, bytes_accessed=13 * 10**6, transcendentals=0),
        name="join",
    )(base, used, got)
    return (
        codes.reshape(layers, 1, 1, per_layer, BLOCK, width),
        scales.reshape(layers, 1, 1, per_layer, width),
    )


def solution(mesh):
    return jax.shard_map(
        shards,
        mesh=mesh,
        in_specs=(P(None, "train", "serve"), P(), P(None, "train", None)),
        out_specs=(P(None, "serve", "train", None, None, None), P(None, "serve", "train", None, None)),
        check_vma=False,
    )
```

time: 292 us -> 152 us (0.52)
  the two profiles are of different devices: /device:TPU:38 before, /device:TPU:123 now
where the time goes in v1:
time: 152 us; the launch traced here: 151 us
  waiting for transfers between devices  99.2 us (65%)
  Pallas kernels  27.8 us (18%)
  starting transfers between devices  14.3 us (9%)
  local copies, waits for them, and re-layouts  9.04 us (6%)
    all_to_all x1, waiting for transfers between devices, shards(): got = lax.all_to_all(sent, 'serve', split_axis=0, concat_axis=0, tiled=True)  99.2 us
    pallas_call x1, Pallas kernels, shards(): pl.pallas_call(functools.partial(join_kernel, slots), grid=(layers,), in_...  11.2 us
    pallas_call x1, Pallas kernels, shards(): pl.pallas_call(turn_kernel, in_specs=[in_smem(), pl.BlockSpec(memory_spac...  9.23 us
    unnamed x14, local copies, waits for them, and re-layouts  9.04 us
    all_to_all x1, starting transfers between devices, shards(): got = lax.all_to_all(sent, 'serve', split_axis=0, concat_axis=0, tiled=True)  6.47 us
    pallas_call x1, Pallas kernels, shards(): pl.pallas_call(functools.partial(pack_kernel, slots), in_specs=[in_smem()...  6.29 us
    ppermute x1, starting transfers between devices, shards(): lax.ppermute(head, 'train', [(i + 1, i) for i in range(train_n - 1)])  3.94 us
    ppermute x1, starting transfers between devices, shards(): left = lax.ppermute(tail, 'train', [(i, i + 1) for i in range(train_n - 1)])  3.88 us
  transfers between devices with their start and end apart: 3, of which 1 were waited for; matrix products, arithmetic and copies ran while one was open for 0% of the time, Pallas kernels for 6%

profile of v1, /device:TPU:123, one launch (start us, length us, event | category | flops | bytes accessed | tf_op | source)
XLA Modules:
  0.0 151.5 jit_solution(12491804825784910178)
XLA Ops:
  0.6 0.0 copy-start.1
  0.6 2.2 %copy-done.1 = bf16[16,960,132]{1,0,2:T(8,128)(2,1)S(1)} copy-done((bf16[16,960,132]{1,0,2:T(8,128)(2,1)S(1)}, bf16[16,960,132]{1,0,2:T(8,128)(2,1)}, u32[]{:S(2)}) %copy-start.1) | copy-done | bytes 4055064
  2.9 0.0 copy-start.2
  2.9 1.0 edges.1
  3.9 0.0 copy-start.6
  3.9 0.0 copy-start.5
  3.9 3.9 %collective-permute-start = (bf16[17,32,128]{2,1,0:T(8,128)(2,1)S(1)}, bf16[17,32,128]{2,1,0:T(8,128)(2,1)S(1)}, u32[]{:S(2)}, u32[]{:S(2)}) collective-permute-start(bf16[17,32,128]{2,1,0:T(8,128)(2,1)S(1)} %get-tuple-element.10), channel_id=1, source_target_pairs={{0,16},{16,32},{32,48},{48,64},{64,80},{80,96},{96,112},{1,17},{17... | collective-permute-start | bytes 417800 | tf_op jit(solution)/shard_map/ppermute | solution.py:236
  7.8 3.9 %collective-permute-start.1 = (bf16[17,32,128]{2,1,0:T(8,128)(2,1)S(1)}, bf16[17,32,128]{2,1,0:T(8,128)(2,1)S(1)}, u32[]{:S(2)}, u32[]{:S(2)}) collective-permute-start(bf16[17,32,128]{2,1,0:T(8,128)(2,1)S(1)} %get-tuple-element.11), channel_id=1, source_target_pairs={{16,0},{32,16},{48,32},{64,48},{80,64},{96,80},{112,96},{17,1},{33... | collective-permute-start | bytes 417800 | tf_op jit(solution)/shard_map/ppermute | solution.py:237
  11.8 0.0 copy-done.2
  11.8 9.2 %turn.1 = (bf16[16,960,128]{2,1,0:T(8,128)(2,1)S(1)}, bf16[960,64]{1,0:T(8,128)(2,1)S(1)}) custom-call(s32[1]{0:T(128)} %bitcast.1.me_ref, bf16[132,16,960]{2,1,0:T(8,128)(2,1)S(1)} %bitcast.11), custom_call_target="tpu_custom_call" | custom-call | flops 3000000000 | bytes 9000000 | tf_op jit(solution)/shard_map/turn/pallas_call | solution.py:239
  21.0 0.0 copy-start.3
  21.0 1.9 %copy-done.3 = bf16[16,960,128]{2,1,0:T(8,128)(2,1)} copy-done((bf16[16,960,128]{2,1,0:T(8,128)(2,1)}, bf16[16,960,128]{2,1,0:T(8,128)(2,1)S(1)}, u32[]{:S(2)}) %copy-start.3) | copy-done | bytes 3932184
  23.0 0.0 copy-done.6
  23.0 0.1 select_reduce_fusion
  23.1 0.0 collective-permute-done.left_ref
  23.1 0.0 collective-permute-done.1.right_ref
  23.1 0.0 copy-done.5
  23.1 0.0 copy-start.4
  23.2 2.1 %copy-done.4 = bf16[16,960,128]{2,1,0:T(8,128)(2,1)S(1)} copy-done((bf16[16,960,128]{2,1,0:T(8,128)(2,1)S(1)}, bf16[16,960,128]{2,1,0:T(8,128)(2,1)}, u32[]{:S(2)}) %copy-start.4) | copy-done | bytes 3932184
  25.3 6.3 %pack.1 = bf16[16,50,32,128]{3,2,1,0:T(8,128)(2,1)S(1)} custom-call(s32[1]{0:T(128)} %bitcast.1.me_ref, s32[16]{0:T(128)S(1)} %get-tuple-element.21.first_ref, s32[16]{0:T(128)S(1)} %get-tuple-element.20.next_ref, s32[16,28]{1,0:T(8,128)S(1)} %bitcast.12, bf16[16,960,128]{2,1,0:T(8,128)(2,1)S(1)} %copy-done.4, ...), custom_call_target="tpu_custom_call" | custom-call | flops 1000000000 | bytes 10000000 | tf_op jit(solution)/shard_map/pack/pallas_call | solution.py:260
  31.6 0.0 copy-start
  31.6 2.8 %copy-done = bf16[16,50,32,128]{3,2,1,0:T(8,128)(2,1)} copy-done((bf16[16,50,32,128]{3,2,1,0:T(8,128)(2,1)}, bf16[16,50,32,128]{3,2,1,0:T(8,128)(2,1)S(1)}, u32[]{:S(2)}) %copy-start) | copy-done | bytes 6553624
  34.3 6.5 %all-to-all-start = ((bf16[16,50,32,128]{3,2,1,0:T(8,128)(2,1)}), bf16[16,50,32,128]{3,2,1,0:T(8,128)(2,1)}, u32[]{:S(2)}, u32[]{:S(2)}) async-start(bf16[16,50,32,128]{3,2,1,0:T(8,128)(2,1)} %copy-done), calls=%async_computation | async-start | bytes 13107200 | tf_op jit(solution)/shard_map/all_to_all | solution.py:271
  40.8 0.1 convert_reduce_fusion.used_ref
  40.9 0.1 select_reduce_fusion.2.base_ref
  41.0 99.2 %all-to-all-done.in_hbm = bf16[16,50,32,128]{3,2,1,0:T(8,128)(2,1)} async-done(((bf16[16,50,32,128]{3,2,1,0:T(8,128)(2,1)}), bf16[16,50,32,128]{3,2,1,0:T(8,128)(2,1)}, u32[]{:S(2)}, u32[]{:S(2)}) %all-to-all-start) | async-done | bytes 6553632 | tf_op jit(solution)/shard_map/all_to_all | solution.py:271
  140.3 11.2 %join.1 = (bf16[16,3,32,2112]{3,2,1,0:T(8,128)(2,1)}, f32[48,1,2112]{2,1,0:T(1,128)}) custom-call(s32[16]{0:T(128)S(1)} %select_reduce_fusion.2.base_ref, s32[16]{0:T(128)S(1)} %convert_reduce_fusion.used_ref, bf16[16,50,32,128]{3,2,1,0:T(8,128)(2,1)} %all-to-all-done.in_hbm), custom_call_target="tpu_custom_call" | custom-call | flops 100000000 | bytes 13000000 | tf_op jit(solution)/shard_map/join/pallas_call | solution.py:276
  (3 shorter events, 0.0 us)
Async XLA Ops:
  0.6 2.2 %copy-start.1 = (bf16[16,960,132]{1,0,2:T(8,128)(2,1)S(1)}, bf16[16,960,132]{1,0,2:T(8,128)(2,1)}, u32[]{:S(2)}) copy-start(bf16[16,960,132]{1,0,2:T(8,128)(2,1)} %param.3) | copy-start | bytes 12165124
  2.9 8.9 %copy-start.2 = (bf16[16,960,132]{1,0,2:T(8,128)(2,1)S(1)}, bf16[16,960,132]{1,0,2:T(8,128)(2,1)}, u32[]{:S(2)}) copy-start(bf16[16,960,132]{1,0,2:T(8,128)(2,1)} %param.3) | copy-start | bytes 12165124
  3.9 19.0 %copy-start.6 = (s32[16,9]{1,0:T(8,128)S(1)}, s32[16,9]{1,0:T(8,128)}, u32[]{:S(2)}) copy-start(s32[16,9]{1,0:T(8,128)} %param.4) | copy-start | bytes 1732
  3.9 19.2 %copy-start.5 = (s32[16,28,1]{1,2,0:T(1,128)S(1)}, s32[16,28,1]{1,2,0:T(1,128)}, u32[]{:S(2)}) copy-start(s32[16,28,1]{1,2,0:T(1,128)} %param.5) | copy-start | bytes 5380
  3.9 19.2 %collective-permute-start = (bf16[17,32,128]{2,1,0:T(8,128)(2,1)S(1)}, bf16[17,32,128]{2,1,0:T(8,128)(2,1)S(1)}, u32[]{:S(2)}, u32[]{:S(2)}) collective-permute-start(bf16[17,32,128]{2,1,0:T(8,128)(2,1)S(1)} %get-tuple-element.10), channel_id=1, source_target_pairs={{0,16},{16,32},{32,48},{48,64},{64,80},{80,96},{96,112},{1,17},{17... | collective-permute-start | bytes 417800 | tf_op jit(solution)/shard_map/ppermute | solution.py:236
  7.8 15.3 %collective-permute-start.1 = (bf16[17,32,128]{2,1,0:T(8,128)(2,1)S(1)}, bf16[17,32,128]{2,1,0:T(8,128)(2,1)S(1)}, u32[]{:S(2)}, u32[]{:S(2)}) collective-permute-start(bf16[17,32,128]{2,1,0:T(8,128)(2,1)S(1)} %get-tuple-element.11), channel_id=1, source_target_pairs={{16,0},{32,16},{48,32},{64,48},{80,64},{96,80},{112,96},{17,1},{33... | collective-permute-start | bytes 417800 | tf_op jit(solution)/shard_map/ppermute | solution.py:237
  21.0 1.9 %copy-start.3 = (bf16[16,960,128]{2,1,0:T(8,128)(2,1)}, bf16[16,960,128]{2,1,0:T(8,128)(2,1)S(1)}, u32[]{:S(2)}) copy-start(bf16[16,960,128]{2,1,0:T(8,128)(2,1)S(1)} %get-tuple-element.8.rows_ref) | copy-start | bytes 11796484
  23.1 2.1 %copy-start.4 = (bf16[16,960,128]{2,1,0:T(8,128)(2,1)S(1)}, bf16[16,960,128]{2,1,0:T(8,128)(2,1)}, u32[]{:S(2)}) copy-start(bf16[16,960,128]{2,1,0:T(8,128)(2,1)} %copy-done.3) | copy-start | bytes 11796484
  31.6 2.8 %copy-start = (bf16[16,50,32,128]{3,2,1,0:T(8,128)(2,1)}, bf16[16,50,32,128]{3,2,1,0:T(8,128)(2,1)S(1)}, u32[]{:S(2)}) copy-start(bf16[16,50,32,128]{3,2,1,0:T(8,128)(2,1)S(1)} %pack.1) | copy-start | bytes 19660804
  34.3 105.9 %all-to-all-start = ((bf16[16,50,32,128]{3,2,1,0:T(8,128)(2,1)}), bf16[16,50,32,128]{3,2,1,0:T(8,128)(2,1)}, u32[]{:S(2)}, u32[]{:S(2)}) async-start(bf16[16,50,32,128]{3,2,1,0:T(8,128)(2,1)} %copy-done), calls=%async_computation | async-start | bytes 13107200 | tf_op jit(solution)/shard_map/all_to_all | solution.py:271

commit v2 on v1

--- a/solution.py
+++ b/solution.py
@@ -5,6 +5,7 @@
 from jax import lax
 from jax.experimental import pallas as pl
 from jax.experimental.pallas import tpu as pltpu
+from jax.sharding import Mesh
 from jax.sharding import PartitionSpec as P
 
 BLOCK = 32
@@ -14,6 +15,8 @@
 NT = (((1,), (1,)), ((), ()))
 F32 = jnp.float32
 BF16 = jnp.bfloat16
+CORES = 2
+SERVE = ("chip", "core")
 MIB = 1024 * 1024
 
 
@@ -64,7 +67,7 @@
     head_ref[PACK], tail_ref[PACK] = turned[:SHIFT], turned[SHIFT:]
 
 
-def turn_kernel(me_ref, x_hbm, rows_ref, rest_ref, x_ref, planes, sems):
+def turn_kernel(me_ref, x_hbm, rows_hbm, rest_ref, x_ref, planes, rows_ref, sems, out_sem):
     length = x_ref.shape[2]
     steps = LANES // PACK
     parts = [pl.ds(PACK * i, PACK) for i in range(steps)] + [pl.ds(LANES, 4)]
@@ -91,23 +94,47 @@
                 identity(size), planes[layer, :, start : start + size], NT, preferred_element_type=F32
             )
             rows_ref[layer, start : start + size, :] = pltpu.roll(turned, shift, 1).astype(BF16)
+        pltpu.make_async_copy(rows_ref.at[layer], rows_hbm.at[layer], out_sem).start()
         return carry
 
     lax.fori_loop(0, PACK, layer_step, 0)
+    pltpu.make_async_copy(rows_ref, rows_hbm, out_sem).wait()
 
 
 def pack_kernel(
-    slots, me_ref, first_ref, next_ref, group_ref, rows_ref, rest_ref, left_ref, right_ref, out_ref, extra, count
+    slots,
+    me_ref,
+    first_ref,
+    next_ref,
+    group_ref,
+    rows_hbm,
+    rest_ref,
+    left_ref,
+    right_ref,
+    own_hbm,
+    other_hbm,
+    rows_ref,
+    out_ref,
+    extra,
+    count,
+    sems,
+    out_sems,
 ):
     layers, blocks = group_ref.shape
+    peers = out_ref.shape[0] // CORES
+    loads = [pltpu.make_async_copy(rows_hbm.at[i], rows_ref.at[i], sems.at[i]) for i in range(layers)]
+    for load in loads:
+        load.start()
     length = rest_ref.shape[0]
     row = iota((BLOCK, LANES), 0)
     lane_group = iota((BLOCK, LANES), 1) // 4
     me = me_ref[0]
+    core = me & 1
     for g in range(out_ref.shape[0]):
         count[g] = 0
 
     def layer_step(layer, carry):
+        pltpu.make_async_copy(rows_hbm.at[layer], rows_ref.at[layer], sems.at[layer]).wait()
         repeat = spread(layer)
         extra[:length] = dot(rest_ref[...], repeat).astype(BF16)
         first, after = first_ref[layer], next_ref[layer] - (blocks - 1) * BLOCK
@@ -126,35 +153,50 @@
             group = group_ref[layer, b]
             j = count[group]
             count[group] = j + 1
-            out_ref[group, j] = block
+            place = ((group & 1) ^ core) * peers + lax.shift_right_logical(group, 1)
+            out_ref[place, j] = block
             tile = slots + lax.shift_right_logical(j, 5)
-            place = (j + me) & 31
-            out_ref[group, tile] = jnp.where(lane_group == place, rest, out_ref[group, tile])
+            out_ref[place, tile] = jnp.where(lane_group == ((j + me) & 31), rest, out_ref[place, tile])
         return carry
 
     lax.fori_loop(0, layers, layer_step, 0)
-
-
-def join_kernel(slots, base_ref, used_ref, in_hbm, codes_ref, scale_ref, held, sems):
-    peers, units = in_hbm.shape[0], in_hbm.shape[1]
+    stores = [
+        pltpu.make_async_copy(out_ref.at[pl.ds(peers * i, peers)], ref, out_sems.at[i])
+        for i, ref in enumerate((own_hbm, other_hbm))
+    ]
+    for store in stores:
+        store.start()
+    for store in stores:
+        store.wait()
+
+
+def join_kernel(slots, me_ref, base_ref, used_ref, own_hbm, other_hbm, codes_ref, scale_ref, held, sems):
+    peers, units = CORES * own_hbm.shape[0], own_hbm.shape[1]
+    core = me_ref[0] & 1
     per_layer = codes_ref.shape[1]
     layer = pl.program_id(0)
     cuts = [(slots, units - slots)] + [(start, min(8, slots - start)) for start in range(0, slots, 8)]
     copies = [
-        pltpu.make_async_copy(in_hbm.at[:, pl.ds(s, n)], held.at[:, pl.ds(s, n)], sems.at[i])
+        [
+            pltpu.make_async_copy(ref.at[:, pl.ds(s, n)], held.at[place, :, pl.ds(s, n)], sems.at[2 * i + h])
+            for h, (ref, place) in enumerate(((own_hbm, core), (other_hbm, 1 - core)))
+        ]
         for i, (s, n) in enumerate(cuts)
     ]
 
     @pl.when(layer == 0)
     def _():
-        for copy in copies:
-            copy.start()
-        copies[0].wait()
+        for pair in copies:
+            for copy in pair:
+                copy.start()
+        for copy in copies[0]:
+            copy.wait()
 
     for i in range(1, len(copies)):
         @pl.when(layer == cuts[i][0] // per_layer)
         def _(i=i):
-            copies[i].wait()
+            for copy in copies[i]:
+                copy.wait()
 
     lane = iota((BLOCK, LANES), 1)
     base, used = base_ref[layer], used_ref[layer]
@@ -169,7 +211,7 @@
             source = (lane // 4 - jj) & 31
             rest = jnp.zeros((BLOCK, LANES), F32)
             for s in range(peers):
-                rest = jnp.where(source == s, held[s, tile].astype(F32), rest)
+                rest = jnp.where(source == s, held[s % CORES, s // CORES, tile].astype(F32), rest)
             rest = pltpu.roll(rest, (LANES - 4 * jj) & (LANES - 1), 1)
             before = None
             for t in range(peers + 1):
@@ -177,7 +219,7 @@
                 if before is not None:
                     x = jnp.where(lane < 4 * t - 4, before, x)
                 if t < peers:
-                    own = held[t, j].astype(F32)
+                    own = held[t % CORES, t // CORES, j].astype(F32)
                     x = own if t == 0 else jnp.where(lane >= 4 * t, own, x)
                     before = own
                 size = min(LANES, width - LANES * t)
@@ -196,15 +238,23 @@
     return pl.BlockSpec(memory_space=pltpu.VMEM)
 
 
+def in_hbm():
+    return pl.BlockSpec(memory_space=pltpu.HBM)
+
+
+def hbm(value):
+    return pltpu.with_memory_space_constraint(value, pltpu.HBM)
+
+
 def in_smem():
     return pl.BlockSpec(memory_space=pltpu.SMEM)
 
 
 def shards(train_weights, row_offset, block_group):
     train_n = lax.axis_size("train")
-    serve_n = lax.axis_size("serve")
+    serve_n = lax.axis_size(SERVE)
     train_idx = lax.axis_index("train")
-    serve_idx = lax.axis_index("serve").astype(jnp.int32)
+    serve_idx = lax.axis_index(SERVE).astype(jnp.int32)
     layers, buffer_len, columns = train_weights.shape
     rows_dev = buffer_len - 2 * SHIFT
     blocks_dev = block_group.shape[1]
@@ -214,7 +264,7 @@
     width = columns * serve_n
     groups = block_group[:, :, 0]
     me = serve_idx.reshape(1)
-    by_column = jnp.transpose(train_weights, (2, 0, 1))
+    by_column = hbm(jnp.transpose(train_weights, (2, 0, 1)))
 
     tile = (columns, layers, LANES)
     edge = jax.ShapeDtypeStruct((layers + 1, SHIFT, LANES), BF16)
@@ -229,7 +279,7 @@
         out_specs=[in_vmem(), in_vmem()],
         out_shape=[edge, edge],
         scratch_shapes=[pltpu.VMEM((layers, LANES, LANES), BF16)],
-        compiler_params=pltpu.CompilerParams(vmem_limit_bytes=16 * MIB),
+        compiler_params=pltpu.CompilerParams(vmem_limit_bytes=8 * MIB),
         cost_estimate=pl.CostEstimate(flops=10**8, bytes_accessed=10**6, transcendentals=0),
         name="edges",
     )(me, by_column, by_column)
@@ -238,18 +288,20 @@
 
     rows, rest = pl.pallas_call(
         turn_kernel,
-        in_specs=[in_smem(), pl.BlockSpec(memory_space=pl.ANY)],
-        out_specs=[in_vmem(), in_vmem()],
+        in_specs=[in_smem(), in_hbm()],
+        out_specs=[in_hbm(), in_vmem()],
         out_shape=[
-            jax.ShapeDtypeStruct((layers, buffer_len, LANES), BF16),
+            pltpu.HBM((layers, buffer_len, LANES), BF16),
             jax.ShapeDtypeStruct((buffer_len, 4 * PACK), BF16),
         ],
         scratch_shapes=[
             pltpu.VMEM((columns, layers, buffer_len), BF16),
             pltpu.VMEM((layers, LANES, buffer_len), BF16),
+            pltpu.VMEM((layers, buffer_len, LANES), BF16),
             pltpu.SemaphoreType.DMA((LANES // PACK + 1,)),
-        ],
-        compiler_params=pltpu.CompilerParams(vmem_limit_bytes=32 * MIB),
+            pltpu.SemaphoreType.DMA,
+        ],
+        compiler_params=pltpu.CompilerParams(vmem_limit_bytes=24 * MIB),
         cost_estimate=pl.CostEstimate(flops=3 * 10**9, bytes_accessed=9 * 10**6, transcendentals=0),
         name="turn",
     )(me, by_column)
@@ -257,18 +309,28 @@
     entries = jnp.arange(train_n + 1, dtype=jnp.int32)
     first_row = jnp.sum(jnp.where(entries[None, :] == train_idx, row_offset, 0), axis=1) - train_idx * rows_dev
     next_row = jnp.sum(jnp.where(entries[None, :] == train_idx + 1, row_offset, 0), axis=1) - train_idx * rows_dev
-    sent = pl.pallas_call(
+    half = pltpu.HBM((serve_n // CORES, units, BLOCK, LANES), BF16)
+    own, other = pl.pallas_call(
         functools.partial(pack_kernel, slots),
-        in_specs=[in_smem()] * 4 + [in_vmem()] * 4,
-        out_specs=in_vmem(),
-        out_shape=jax.ShapeDtypeStruct((serve_n, units, BLOCK, LANES), BF16),
-        scratch_shapes=[pltpu.VMEM((buffer_len, LANES), BF16), pltpu.SMEM((serve_n,), jnp.int32)],
+        in_specs=[in_smem()] * 4 + [in_hbm()] + [in_vmem()] * 3,
+        out_specs=[in_hbm()] * CORES,
+        out_shape=[half] * CORES,
+        scratch_shapes=[
+            pltpu.VMEM((layers, buffer_len, LANES), BF16),
+            pltpu.VMEM((serve_n, units, BLOCK, LANES), BF16),
+            pltpu.VMEM((buffer_len, LANES), BF16),
+            pltpu.SMEM((serve_n,), jnp.int32),
+            pltpu.SemaphoreType.DMA((layers,)),
+            pltpu.SemaphoreType.DMA((CORES,)),
+        ],
         compiler_params=pltpu.CompilerParams(vmem_limit_bytes=24 * MIB),
         cost_estimate=pl.CostEstimate(flops=10**9, bytes_accessed=10**7, transcendentals=0),
         name="pack",
-    )(me, first_row, next_row, groups, rows, rest, left, right)
-
-    got = lax.all_to_all(sent, "serve", split_axis=0, concat_axis=0, tiled=True)
+    )(me, first_row, next_row, groups, hbm(rows), rest, left, right)
+
+    from_own = lax.all_to_all(own, "chip", split_axis=0, concat_axis=0, tiled=True)
+    passed = lax.ppermute(other, "core", [(0, 1), (1, 0)])
+    from_other = lax.all_to_all(passed, "chip", split_axis=0, concat_axis=0, tiled=True)
 
     used = jnp.sum((groups == serve_idx).astype(jnp.int32), axis=1)
     order = jnp.arange(layers, dtype=jnp.int32)
@@ -276,7 +338,7 @@
     codes, scales = pl.pallas_call(
         functools.partial(join_kernel, slots),
         grid=(layers,),
-        in_specs=[in_smem(), in_smem(), pl.BlockSpec(memory_space=pl.ANY)],
+        in_specs=[in_smem()] * 3 + [in_hbm()] * CORES,
         out_specs=[
             pl.BlockSpec((1, per_layer, BLOCK, width), lambda i: (i, 0, 0, 0)),
             pl.BlockSpec((per_layer, 1, width), lambda i: (i, 0, 0)),
@@ -286,15 +348,15 @@
             jax.ShapeDtypeStruct((layers * per_layer, 1, width), F32),
         ],
         scratch_shapes=[
-            pltpu.VMEM((serve_n, units, BLOCK, LANES), BF16),
-            pltpu.SemaphoreType.DMA((1 + -(-slots // 8),)),
+            pltpu.VMEM((CORES, serve_n // CORES, units, BLOCK, LANES), BF16),
+            pltpu.SemaphoreType.DMA((CORES * (1 + -(-slots // 8)),)),
         ],
         compiler_params=pltpu.CompilerParams(
             dimension_semantics=("arbitrary",), vmem_limit_bytes=24 * MIB
         ),
         cost_estimate=pl.CostEstimate(flops=10**8, bytes_accessed=13 * 10**6, transcendentals=0),
         name="join",
-    )(base, used, got)
+    )(me, base, used, hbm(from_own), hbm(from_other))
     return (
         codes.reshape(layers, 1, 1, per_layer, BLOCK, width),
         scales.reshape(layers, 1, 1, per_layer, width),
@@ -302,10 +364,14 @@
 
 
 def solution(mesh):
+    cores = Mesh(
+        mesh.devices.reshape(mesh.shape["train"], mesh.shape["serve"] // CORES, CORES),
+        ("train", *SERVE),
+    )
     return jax.shard_map(
         shards,
-        mesh=mesh,
-        in_specs=(P(None, "train", "serve"), P(), P(None, "train", None)),
-        out_specs=(P(None, "serve", "train", None, None, None), P(None, "serve", "train", None, None)),
+        mesh=cores,
+        in_specs=(P(None, "train", SERVE), P(), P(None, "train", None)),
+        out_specs=(P(None, SERVE, "train", None, None, None), P(None, SERVE, "train", None, None)),
         check_vma=False,
     )

time: 152 us -> 132 us (0.87)
  the two profiles are of different devices: /device:TPU:123 before, /device:TPU:38 now
where the time goes in v2:
time: 132 us; the launch traced here: 131 us
  blocking collectives  44.9 us (34%)
  waiting for transfers between devices  37.2 us (28%)
  Pallas kernels  34.3 us (26%)
  starting transfers between devices  13.2 us (10%)
    all_to_all x1, blocking collectives, shards(): lax.all_to_all(own, 'chip', split_axis=0, concat_axis=0, tiled=True)  44.9 us
    all_to_all x1, waiting for transfers between devices, shards(): lax.all_to_all(passed, 'chip', split_axis=0, concat_axis=0, tiled=True)  37.2 us
    pallas_call x1, Pallas kernels, shards(): pl.pallas_call(functools.partial(join_kernel, slots), grid=(layers,), in_...  11.4 us
    pallas_call x1, Pallas kernels, shards(): pl.pallas_call(turn_kernel, in_specs=[in_smem(), in_hbm()], out_specs=[in...  10.5 us
    pallas_call x1, Pallas kernels, shards(): pl.pallas_call(functools.partial(pack_kernel, slots), in_specs=[in_smem()...  10.3 us
    all_to_all x1, starting transfers between devices, shards(): lax.all_to_all(passed, 'chip', split_axis=0, concat_axis=0, tiled=True)  5.72 us
    ppermute x1, starting transfers between devices, shards(): left = lax.ppermute(tail, 'train', [(i, i + 1) for i in range(train_n - 1)])  4.67 us
    ppermute x1, starting transfers between devices, shards(): lax.ppermute(head, 'train', [(i + 1, i) for i in range(train_n - 1)])  2.68 us
  transfers between devices with their start and end apart: 4, of which 1 were waited for; matrix products, arithmetic and copies ran while one was open for 0% of the time, Pallas kernels for 8%

profile of v2, /device:TPU:38, one launch (start us, length us, event | category | flops | bytes accessed | tf_op | source)
XLA Modules:
  0.0 130.7 jit_solution(14350588143533289273)
XLA Ops:
  0.6 2.1 %edges.1 = (bf16[17,32,128]{2,1,0:T(8,128)(2,1)S(1)}, bf16[17,32,128]{2,1,0:T(8,128)(2,1)S(1)}) custom-call(s32[1]{0:T(128)} %bitcast.me_ref, bf16[132,16,960]{2,1,0:T(8,128)(2,1)} %bitcast.11, bf16[132,16,960]{2,1,0:T(8,128)(2,1)} %bitcast.12), custom_call_target="tpu_custom_call" | custom-call | flops 100000000 | bytes 1000000 | tf_op jit(solution)/shard_map/edges/pallas_call | solution.py:271
  2.8 4.7 %collective-permute-start = (bf16[17,32,128]{2,1,0:T(8,128)(2,1)S(1)}, bf16[17,32,128]{2,1,0:T(8,128)(2,1)S(1)}, u32[]{:S(2)}, u32[]{:S(2)}) collective-permute-start(bf16[17,32,128]{2,1,0:T(8,128)(2,1)S(1)} %get-tuple-element.12), channel_id=1, source_target_pairs={{0,16},{16,32},{32,48},{48,64},{64,80},{80,96},{96,112},{1,17},{17... | collective-permute-start | bytes 417800 | tf_op jit(solution)/shard_map/ppermute | solution.py:286
  7.4 0.0 copy-start.1
  7.4 0.0 copy-start
  7.5 2.7 %collective-permute-start.1 = (bf16[17,32,128]{2,1,0:T(8,128)(2,1)S(1)}, bf16[17,32,128]{2,1,0:T(8,128)(2,1)S(1)}, u32[]{:S(2)}, u32[]{:S(2)}) collective-permute-start(bf16[17,32,128]{2,1,0:T(8,128)(2,1)S(1)} %get-tuple-element.13), channel_id=1, source_target_pairs={{16,0},{32,16},{48,32},{64,48},{80,64},{96,80},{112,96},{17,1},{33... | collective-permute-start | bytes 417800 | tf_op jit(solution)/shard_map/ppermute | solution.py:287
  10.1 10.5 %turn.1 = (bf16[16,960,128]{2,1,0:T(8,128)(2,1)}, bf16[960,64]{1,0:T(8,128)(2,1)S(1)}) custom-call(s32[1]{0:T(128)} %bitcast.me_ref, bf16[132,16,960]{2,1,0:T(8,128)(2,1)} %bitcast.13), custom_call_target="tpu_custom_call" | custom-call | flops 3000000000 | bytes 9000000 | tf_op jit(solution)/shard_map/turn/pallas_call | solution.py:289
  20.7 0.0 copy-done.1
  20.7 0.1 select_reduce_fusion
  20.8 0.0 collective-permute-done.left_ref
  20.8 0.0 collective-permute-done.1.right_ref
  20.8 0.0 copy-done
  20.8 10.3 %pack.1 = (bf16[8,50,32,128]{3,2,1,0:T(8,128)(2,1)}, bf16[8,50,32,128]{3,2,1,0:T(8,128)(2,1)}) custom-call(s32[1]{0:T(128)} %bitcast.me_ref, s32[16]{0:T(128)S(1)} %get-tuple-element.25.first_ref, s32[16]{0:T(128)S(1)} %get-tuple-element.24.next_ref, s32[16,28]{1,0:T(8,128)S(1)} %bitcast.9, bf16[16,960,128]{2,1,0:T(8,128)(2,1)} %get-tuple-element.10.rows_hbm, ...), custom_call_target="tpu_custom_call" | custom-call | flops 1000000000 | bytes 10000000 | tf_op jit(solution)/shard_map/pack/pallas_call | solution.py:313
  31.1 0.1 collective-permute-start.2
  31.2 44.9 %all_to_all.10.own_hbm = bf16[8,50,32,128]{3,2,1,0:T(8,128)(2,1)} all-to-all(bf16[8,50,32,128]{3,2,1,0:T(8,128)(2,1)} %get-tuple-element.14), channel_id=1, replica_groups=mesh['train'=8,'chip'=8,'core'=2] {'chip'}, dimensions={0} | all-to-all | bytes 6553600 | tf_op jit(solution)/shard_map/all_to_all | solution.py:331
  76.1 0.0 collective-permute-done.2
  76.1 5.7 %all-to-all-start.1 = ((bf16[8,50,32,128]{3,2,1,0:T(8,128)(2,1)}), bf16[8,50,32,128]{3,2,1,0:T(8,128)(2,1)}, u32[]{:S(2)}, u32[]{:S(2)}) async-start(bf16[8,50,32,128]{3,2,1,0:T(8,128)(2,1)} %collective-permute-done.2), calls=%async_computation.1 | async-start | bytes 6553600 | tf_op jit(solution)/shard_map/all_to_all | solution.py:333
  81.8 0.1 convert_reduce_fusion.used_ref
  82.0 0.1 select_reduce_fusion.2.base_ref
  82.1 37.2 %all-to-all-done.1.other_hbm = bf16[8,50,32,128]{3,2,1,0:T(8,128)(2,1)} async-done(((bf16[8,50,32,128]{3,2,1,0:T(8,128)(2,1)}), bf16[8,50,32,128]{3,2,1,0:T(8,128)(2,1)}, u32[]{:S(2)}, u32[]{:S(2)}) %all-to-all-start.1) | async-done | bytes 3276832 | tf_op jit(solution)/shard_map/all_to_all | solution.py:333
  119.3 11.4 %join.1 = (bf16[16,3,32,2112]{3,2,1,0:T(8,128)(2,1)}, f32[48,1,2112]{2,1,0:T(1,128)}) custom-call(s32[1]{0:T(128)} %bitcast.me_ref, s32[16]{0:T(128)S(1)} %select_reduce_fusion.2.base_ref, s32[16]{0:T(128)S(1)} %convert_reduce_fusion.used_ref, bf16[8,50,32,128]{3,2,1,0:T(8,128)(2,1)} %all_to_all.10.own_hbm, bf16[8,50,32,128]{3,2,1,0:T(8,128)(2,1)} %all-to-all-done.1.other_hbm), custom_call_target="tpu_custom_call" | custom-call | flops 100000000 | bytes 13000000 | tf_op jit(solution)/shard_map/join/pallas_call | solution.py:338
  (3 shorter events, 0.0 us)
Async XLA Ops:
  2.8 18.1 %collective-permute-start = (bf16[17,32,128]{2,1,0:T(8,128)(2,1)S(1)}, bf16[17,32,128]{2,1,0:T(8,128)(2,1)S(1)}, u32[]{:S(2)}, u32[]{:S(2)}) collective-permute-start(bf16[17,32,128]{2,1,0:T(8,128)(2,1)S(1)} %get-tuple-element.12), channel_id=1, source_target_pairs={{0,16},{16,32},{32,48},{48,64},{64,80},{80,96},{96,112},{1,17},{17... | collective-permute-start | bytes 417800 | tf_op jit(solution)/shard_map/ppermute | solution.py:286
  7.4 13.2 %copy-start.1 = (s32[16,9]{1,0:T(8,128)S(1)}, s32[16,9]{1,0:T(8,128)}, u32[]{:S(2)}) copy-start(s32[16,9]{1,0:T(8,128)} %param.4) | copy-start | bytes 1732
  7.4 13.4 %copy-start = (s32[16,28,1]{1,2,0:T(1,128)S(1)}, s32[16,28,1]{1,2,0:T(1,128)}, u32[]{:S(2)}) copy-start(s32[16,28,1]{1,2,0:T(1,128)} %param.5) | copy-start | bytes 5380
  7.5 13.4 %collective-permute-start.1 = (bf16[17,32,128]{2,1,0:T(8,128)(2,1)S(1)}, bf16[17,32,128]{2,1,0:T(8,128)(2,1)S(1)}, u32[]{:S(2)}, u32[]{:S(2)}) collective-permute-start(bf16[17,32,128]{2,1,0:T(8,128)(2,1)S(1)} %get-tuple-element.13), channel_id=1, source_target_pairs={{16,0},{32,16},{48,32},{64,48},{80,64},{96,80},{112,96},{17,1},{33... | collective-permute-start | bytes 417800 | tf_op jit(solution)/shard_map/ppermute | solution.py:287
  31.1 45.0 %collective-permute-start.2 = (bf16[8,50,32,128]{3,2,1,0:T(8,128)(2,1)}, bf16[8,50,32,128]{3,2,1,0:T(8,128)(2,1)}, u32[]{:S(2)}, u32[]{:S(2)}) collective-permute-start(bf16[8,50,32,128]{3,2,1,0:T(8,128)(2,1)} %get-tuple-element.15), channel_id=1, source_target_pairs={{0,1},{1,0},{2,3},{3,2},{4,5},{5,4},{6,7},{7,6},{8,9},{9,8},{10,11... | collective-permute-start | bytes 9830408 | tf_op jit(solution)/shard_map/ppermute | solution.py:332
  76.1 43.2 %all-to-all-start.1 = ((bf16[8,50,32,128]{3,2,1,0:T(8,128)(2,1)}), bf16[8,50,32,128]{3,2,1,0:T(8,128)(2,1)}, u32[]{:S(2)}, u32[]{:S(2)}) async-start(bf16[8,50,32,128]{3,2,1,0:T(8,128)(2,1)} %collective-permute-done.2), calls=%async_computation.1 | async-start | bytes 6553600 | tf_op jit(solution)/shard_map/all_to_all | solution.py:333
